TPU v7x, 32 devices: a whole 2x2x4 slice. The times are simulated.
32 devices in a mesh: pair: 4 (over y, x), aux: 8 (over z, core).
Axes of the slice: x: 2, y: 2, z: 4, core: 2. Of those that a mesh axis runs over, the one named last changes fastest.
Arguments:
- same_panels: bfloat16 [32, 2, 112, 59904], P('aux', None, None, 'pair'), may hold values from -1 to 1
- opposite_panels: bfloat16 [32, 2, 112, 59904], P('aux', None, None, 'pair'), may hold values from -1 to 1
- same_amplitudes: bfloat16 [32, 112, 112], replicated, may hold values from -2 to 2
- opposite_amplitudes: bfloat16 [32, 112, 112], replicated, may hold values from -2 to 2
- same_energies: float32 [32, 2, 112], replicated, may hold values from 0.5 to 3
- opposite_energies: float32 [32, 2, 112], replicated, may hold values from 0.5 to 3
- same_ranks: int32 [32], replicated, may hold values from 48 to 112
- opposite_ranks: int32 [32], replicated, may hold values from 48 to 112
Outputs:
- same_residual: float32 [32, 112, 112], P('pair', 'aux')
- opposite_residual: float32 [32, 112, 112], P('pair', 'aux')
Inputs may be any that keep to these rules, and one draw needn't show every extreme that they name: `same_ranks`: slots at or beyond a pair's rank are padding. `opposite_ranks`: slots at or beyond a pair's rank are padding.
All inputs are finite; a program needn't handle non-finite values.
Results may differ from a plain program's by a relative error of at most 0.0013.
Values may be sent and summed in bfloat16 or wider, within the bound.
No kernel may reach another device: no remote copies, remote signals or barrier semaphores. Data moves between devices by JAX's collectives and lax.ppermute only.
A program may use at most 128 MiB of HBM per device.

v0:
```python
import jax
import jax.numpy as jnp
from jax import lax
from jax.sharding import PartitionSpec as P


def slot_mask(ranks, slots):
    places = jnp.arange(slots, dtype=jnp.int32)
    return (places[None, :] < ranks[:, None]).astype(jnp.float32)


def masked_amplitudes(amplitudes, keep):
    outer = keep[:, :, None] * keep[:, None, :]
    return (amplitudes.astype(jnp.float32) * outer).astype(jnp.bfloat16)


def dressing_total(panels, masked):
    mixed = jnp.einsum("pab,pbn->pan", masked, panels[:, 1], preferred_element_type=jnp.float32)
    return jnp.sum(panels[:, 0].astype(jnp.float32) * mixed, axis=(0, 1))


def partial_terms(panels, coupling):
    exchange = jnp.einsum(
        "pan,pbn->pab", panels[:, 0], panels[:, 1], preferred_element_type=jnp.float32
    )
    scaled = (panels[:, 0].astype(jnp.float32) * coupling[None, None, :]).astype(jnp.bfloat16)
    coulomb = jnp.einsum("pan,pbn->pab", scaled, panels[:, 1], preferred_element_type=jnp.float32)
    return exchange + coulomb


def finish_rows(summed, amplitudes, energies, ranks, pair_start, row_start):
    count = summed.shape[0]
    rows = summed.shape[1]
    slots = amplitudes.shape[1]
    keep = slot_mask(lax.dynamic_slice_in_dim(ranks, pair_start, count, 0), slots)
    amplitude = lax.dynamic_slice_in_dim(amplitudes, pair_start, count, 0)
    masked = masked_amplitudes(amplitude, keep)
    masked_rows = lax.dynamic_slice_in_dim(masked, row_start, rows, 1).astype(jnp.float32)
    energy = lax.dynamic_slice_in_dim(energies, pair_start, count, 0)
    first_gap = lax.dynamic_slice_in_dim(energy[:, 0], row_start, rows, 1)
    keep_rows = lax.dynamic_slice_in_dim(keep, row_start, rows, 1)
    diagonal = (first_gap[:, :, None] + energy[:, 1][:, None, :]) * masked_rows
    return (summed + diagonal) * (keep_rows[:, :, None] * keep[:, None, :])


def local_masked(amplitudes, ranks, start, count):
    slots = amplitudes.shape[1]
    keep = slot_mask(lax.dynamic_slice_in_dim(ranks, start, count, 0), slots)
    return masked_amplitudes(lax.dynamic_slice_in_dim(amplitudes, start, count, 0), keep)


def body(
    same_panels,
    opposite_panels,
    same_amplitudes,
    opposite_amplitudes,
    same_energies,
    opposite_energies,
    same_ranks,
    opposite_ranks,
):
    block_count = same_panels.shape[0]
    pair_index = lax.axis_index("pair")
    aux_index = lax.axis_index("aux")
    owned = block_count * lax.axis_size("aux") // lax.axis_size("pair")
    rows = same_amplitudes.shape[1] // lax.axis_size("aux")
    start = aux_index * block_count
    same_masked = local_masked(same_amplitudes, same_ranks, start, block_count)
    opposite_masked = local_masked(opposite_amplitudes, opposite_ranks, start, block_count)
    partial_coupling = dressing_total(same_panels, same_masked) + dressing_total(
        opposite_panels, opposite_masked
    )
    coupling = lax.psum(partial_coupling, "aux")
    same_rows, opposite_rows = (
        lax.all_to_all(
            partial_terms(same_panels, coupling), "aux", split_axis=1, concat_axis=0, tiled=True
        ),
        lax.all_to_all(
            partial_terms(opposite_panels, coupling), "aux", split_axis=1, concat_axis=0, tiled=True
        ),
    )
    same_sum, opposite_sum = (
        lax.psum_scatter(same_rows, "pair", scatter_dimension=0, tiled=True),
        lax.psum_scatter(opposite_rows, "pair", scatter_dimension=0, tiled=True),
    )
    pair_start = pair_index * owned
    row_start = aux_index * rows
    same_residual = finish_rows(
        same_sum, same_amplitudes, same_energies, same_ranks, pair_start, row_start
    )
    opposite_residual = finish_rows(
        opposite_sum, opposite_amplitudes, opposite_energies, opposite_ranks, pair_start, row_start
    )
    return (same_residual, opposite_residual)


def solution(mesh):
    placed = (
        P("aux", None, None, "pair"),
        P("aux", None, None, "pair"),
        P(),
        P(),
        P(),
        P(),
        P(),
        P(),
    )
    return jax.shard_map(
        body,
        mesh=mesh,
        in_specs=placed,
        out_specs=(P("pair", "aux", None), P("pair", "aux", None)),
        check_vma=False,
    )
```

profile of v0, /device:TPU:0, one launch (start us, length us, event | category | flops | bytes accessed | tf_op | source)
XLA Modules:
  0.0 178.4 jit_solution(11435442703354790816)
XLA Ops:
  7.2 0.7 dynamic_slice.49
  7.9 0.1 fusion.52
  8.0 0.7 dynamic_slice.51
  8.7 0.1 fusion.53
  8.8 10.7 %fusion = f32[14976]{0:T(1024)S(1)} fusion(bf16[4,2,112,14976]{3,2,1,0:T(8,128)(2,1)} %param.8, f32[4,112]{1,0:T(4,128)S(1)} %fusion.52, bf16[32,112,112]{2,1,0:T(8,128)(2,1)} %param.10, s32[]{:T(128)S(6)} %select_n.6), kind=kOutput, calls=%fused_computation.4 | convolution fusion | flops 1523185024 | bytes 27015684 | tf_op jit(solution)/shard_map/pab,pbn->pan/dot_general | solution.py:18
  19.5 10.8 %fusion.2 = f32[14976]{0:T(1024)S(1)} fusion(bf16[4,2,112,14976]{3,2,1,0:T(8,128)(2,1)} %param.9, f32[4,112]{1,0:T(4,128)S(1)} %fusion.53, bf16[32,112,112]{2,1,0:T(8,128)(2,1)} %param.11, s32[]{:T(128)S(6)} %select_n.6), kind=kOutput, calls=%fused_computation.6 | convolution fusion | flops 1523185024 | bytes 27015684 | tf_op jit(solution)/shard_map/pab,pbn->pan/dot_general | solution.py:18
  30.3 30.8 %psum.7 = f32[14976]{0:T(1024)S(1)} all-reduce(f32[14976]{0:T(1024)S(1)} %add.78), channel_id=1, replica_groups=mesh['pair'=4,'aux'=8] {'aux'}, use_global_device_ids=true, to_apply=%region_2.0 | all-reduce | flops 14976 | bytes 119808 | tf_op jit(solution)/shard_map/psum | solution.py:73
  61.1 10.6 %fusion.6 = f32[4,112,112]{2,1,0:T(8,128)S(1)} fusion(f32[14976]{0:T(1024)S(1)} %psum.7, bf16[4,2,112,14976]{3,2,1,0:T(8,128)(2,1)} %param.8), kind=kOutput, calls=%fused_computation.9 | convolution fusion | flops 1522999296 | bytes 27097600 | tf_op jit(solution)/shard_map/pan,pbn->pab/dot_general | solution.py:27
  71.7 10.6 %fusion.32 = f32[4,112,112]{2,1,0:T(8,128)S(1)} fusion(f32[4,112,112]{2,1,0:T(8,128)S(1)} %fusion.6, bf16[4,2,112,14976]{3,2,1,0:T(8,128)(2,1)} %param.8), kind=kOutput, calls=%fused_computation.34 | convolution fusion | flops 1502921728 | bytes 27238400 | tf_op jit(solution)/shard_map/pan,pbn->pab/dot_general | solution.py:23
  82.3 0.0 copy-start
  82.3 0.8 copy.64
  83.1 3.6 %all-to-all-start = ((f32[4,112,112]{2,0,1:T(4,128)}), f32[4,112,112]{2,0,1:T(4,128)S(1)}, u32[]{:S(2)}, u32[]{:S(2)}) async-start(f32[4,112,112]{2,0,1:T(4,128)} %copy.64), calls=%async_computation | async-start | bytes 458752 | tf_op jit(solution)/shard_map/all_to_all | solution.py:75
  86.7 10.6 %fusion.4 = f32[4,112,112]{2,1,0:T(8,128)S(1)} fusion(f32[14976]{0:T(1024)S(1)} %psum.7, bf16[4,2,112,14976]{3,2,1,0:T(8,128)(2,1)} %param.9), kind=kOutput, calls=%fused_computation.8 | convolution fusion | flops 1522999296 | bytes 27097600 | tf_op jit(solution)/shard_map/pan,pbn->pab/dot_general | solution.py:27
  97.3 0.0 copy-start.1
  97.3 0.0 copy-done
  97.3 0.1 dynamic_slice.55
  97.4 0.1 fusion.48
  97.5 10.6 %fusion.37 = f32[4,112,112]{2,1,0:T(8,128)S(1)} fusion(f32[4,112,112]{2,1,0:T(8,128)S(1)} %fusion.4, bf16[4,2,112,14976]{3,2,1,0:T(8,128)(2,1)} %param.9), kind=kOutput, calls=%fused_computation.35 | convolution fusion | flops 1502921728 | bytes 27238400 | tf_op jit(solution)/shard_map/pan,pbn->pab/dot_general | solution.py:23
  108.1 0.1 constant_dynamic-slice_fusion.7
  108.2 0.7 constant_dynamic-slice_fusion.11
  108.9 0.0 copy-done.1
  108.9 0.1 dynamic_slice.61
  109.0 0.8 copy.71
  109.7 0.8 constant_dynamic-slice_fusion.5
  110.5 0.1 fusion.49
  110.6 0.0 all-to-all-done
  110.6 4.8 %all-to-all-start.1 = ((f32[4,112,112]{2,0,1:T(4,128)}), f32[4,112,112]{2,0,1:T(4,128)S(1)}, u32[]{:S(2)}, u32[]{:S(2)}) async-start(f32[4,112,112]{2,0,1:T(4,128)} %copy.71), calls=%async_computation.2 | async-start | bytes 458752 | tf_op jit(solution)/shard_map/all_to_all | solution.py:78
  115.4 0.0 reduce-scatter.3.cloned.1.call-start
  115.5 0.7 copy.65
  116.2 0.0 reduce-scatter.3.cloned.1.call-update
  116.2 0.0 reduce-scatter.5.cloned.1.call-start
  116.3 0.1 constant_dynamic-slice_fusion.2
  116.4 0.1 copy.76
  116.5 0.1 copy.69
  116.6 0.1 copy.70
  116.6 0.1 copy.67
  116.7 0.1 copy.77
  116.8 0.1 copy.74
  116.9 1.0 constant_dynamic-slice_fusion.4
  117.9 1.0 constant_dynamic-slice_fusion.9
  118.8 5.6 %all-to-all-done.1 = f32[4,112,112]{2,0,1:T(4,128)S(1)} async-done(((f32[4,112,112]{2,0,1:T(4,128)}), f32[4,112,112]{2,0,1:T(4,128)S(1)}, u32[]{:S(2)}, u32[]{:S(2)}) %all-to-all-start.1) | async-done | bytes 200736 | tf_op jit(solution)/shard_map/all_to_all | solution.py:78
  124.4 0.7 copy.72
  125.2 0.0 reduce-scatter.5.cloned.1.call-update
  125.2 0.7 constant_dynamic-slice_fusion.6
  125.9 17.9 %reduce-scatter.3.cloned.1.call-done = f32[8,14,112]{2,0,1:T(8,128)} async-done(((f32[32,14,112]{2,0,1:T(8,128)}), f32[8,14,112]{2,0,1:T(8,128)}) %reduce-scatter.3.cloned.1.call-update) | async-done | bytes 50192 | tf_op jit(solution)/shard_map/reduce_scatter | solution.py:83
  143.9 1.6 multiply_multiply_fusion.1
  145.4 24.6 %reduce-scatter.5.cloned.1.call-done = f32[8,14,112]{2,0,1:T(8,128)} async-done(((f32[32,14,112]{2,0,1:T(8,128)}), f32[8,14,112]{2,0,1:T(8,128)}) %reduce-scatter.5.cloned.1.call-update) | async-done | bytes 50192 | tf_op jit(solution)/shard_map/reduce_scatter | solution.py:84
  170.1 1.6 multiply_multiply_fusion
  (3 shorter events, 0.0 us)
Async XLA Ops:
  82.3 15.0 %copy-start = (s32[32]{0:T(128)S(1)}, s32[32]{0:T(128)}, u32[]{:S(2)}) copy-start(s32[32]{0:T(128)} %param.14) | copy-start | bytes 388
  83.1 27.5 %all-to-all-start = ((f32[4,112,112]{2,0,1:T(4,128)}), f32[4,112,112]{2,0,1:T(4,128)S(1)}, u32[]{:S(2)}, u32[]{:S(2)}) async-start(f32[4,112,112]{2,0,1:T(4,128)} %copy.64), calls=%async_computation | async-start | bytes 458752 | tf_op jit(solution)/shard_map/all_to_all | solution.py:75
  97.3 11.6 %copy-start.1 = (s32[32]{0:T(128)S(1)}, s32[32]{0:T(128)}, u32[]{:S(2)}) copy-start(s32[32]{0:T(128)} %param.15) | copy-start | bytes 388
  110.6 13.8 %all-to-all-start.1 = ((f32[4,112,112]{2,0,1:T(4,128)}), f32[4,112,112]{2,0,1:T(4,128)S(1)}, u32[]{:S(2)}, u32[]{:S(2)}) async-start(f32[4,112,112]{2,0,1:T(4,128)} %copy.71), calls=%async_computation.2 | async-start | bytes 458752 | tf_op jit(solution)/shard_map/all_to_all | solution.py:78
  115.4 28.4 %reduce-scatter.3.cloned.1.call-start = ((), (), s32[]{:S(2)}) async-start(), calls=%async_computation.4 | async-start | bytes 286720 | tf_op jit(solution)/shard_map/reduce_scatter | solution.py:83
  116.2 53.8 %reduce-scatter.5.cloned.1.call-start = ((), (), s32[]{:S(2)}) async-start(), calls=%async_computation.5 | async-start | bytes 286720 | tf_op jit(solution)/shard_map/reduce_scatter | solution.py:84
Sparse Core Ops, SparseCore 0:
  119.0 24.7 reduce-scatter.2
  146.7 23.3 reduce-scatter.4
where the time goes:
time: 179 us; the launch traced here: 178 us
  matrix products  63.9 us (36%)
  waiting for transfers between devices  48.2 us (27%)
  blocking collectives  30.8 us (17%)
  between operations  14.2 us (8%)
  local copies, waits for them, and re-layouts  9.48 us (5%)
  starting transfers between devices  8.49 us (5%)
  other arithmetic  3.41 us (2%)
    psum x1, blocking collectives, body(): coupling = lax.psum(partial_coupling, 'aux')  30.8 us
    reduce_scatter x1, waiting for transfers between devices, body(): lax.psum_scatter(opposite_rows, 'pair', scatter_dimension=0, tiled=True)  24.6 us
    dot_general x2, matrix products, dressing_total(): jnp.einsum('pab,pbn->pan', masked, panels[:, 1], preferred_element_type=j...  21.5 us
    dot_general x2, matrix products, partial_terms(): jnp.einsum('pan,pbn->pab', panels[:, 0], panels[:, 1], preferred_element_...  21.2 us
    dot_general x2, matrix products, partial_terms(): jnp.einsum('pan,pbn->pab', scaled, panels[:, 1], preferred_element_type=j...  21.2 us
    reduce_scatter x1, waiting for transfers between devices, body(): lax.psum_scatter(same_rows, 'pair', scatter_dimension=0, tiled=True)  17.9 us
    all_to_all x1, waiting for transfers between devices, body(): lax.all_to_all(partial_terms(opposite_panels, coupling), 'aux', split_axi...  5.62 us
    all_to_all x1, starting transfers between devices, body(): lax.all_to_all(partial_terms(opposite_panels, coupling), 'aux', split_axi...  4.83 us
  transfers between devices with their start and end apart: 4, of which 3 were waited for; matrix products, arithmetic and copies ran while one was open for 17% of the time, Pallas kernels for 0%

commit v1 on v0

v1 whole, which is shorter than its diff:
```python
import functools

import jax
import jax.numpy as jnp
from jax import lax
from jax.experimental import pallas as pl
from jax.experimental.pallas import tpu as pltpu
from jax.sharding import PartitionSpec as P

STEP = 256
SMALL = 8 * 1024 * 1024
ROW_BY_ROW = (((1,), (1,)), ((), ()))

ANYWHERE = pl.BlockSpec(memory_space=pltpu.HBM)
SCALARS = pl.BlockSpec(memory_space=pltpu.SMEM)
ON_CHIP = pl.BlockSpec(memory_space=pltpu.VMEM)


def pieces(total, step):
    return [(at, min(step, total - at)) for at in range(0, total, step)]


def call(kernel, outs, ins, scratch=(), flops=0, name=None):
    placed = [
        value if spec is not ON_CHIP else pltpu.with_memory_space_constraint(value, pltpu.VMEM)
        for spec, value in ins
    ]
    return pl.pallas_call(
        kernel,
        out_shape=tuple(pltpu.VMEM(shape, dtype) for shape, dtype in outs),
        in_specs=[spec for spec, _ in ins],
        out_specs=(ON_CHIP,) * len(outs),
        scratch_shapes=list(scratch),
        compiler_params=pltpu.CompilerParams(vmem_limit_bytes=SMALL),
        cost_estimate=pl.CostEstimate(flops=flops, bytes_accessed=0, transcendentals=0),
        name=name,
    )(*placed)


def mask(rank, slots):
    rows = lax.broadcasted_iota(jnp.int32, (slots, slots), 0) < rank
    columns = lax.broadcasted_iota(jnp.int32, (slots, slots), 1) < rank
    return jnp.logical_and(rows, columns)


def dressing_kernel(
    places,
    same_ranks,
    opposite_ranks,
    same_ref,
    opposite_ref,
    same_amp_ref,
    opposite_amp_ref,
    same_energy_ref,
    opposite_energy_ref,
    same_held,
    opposite_held,
    coupling_ref,
    base_ref,
    amp,
    energy,
    masked,
    total,
    panel_sem,
    small_sem,
):
    count, _, slots, functions = same_held.shape
    start = places[0]
    sources = (same_ref, opposite_ref)
    held = (same_held, opposite_held)
    small_copies = [
        pltpu.make_async_copy(
            source.at[pl.ds(start, count)], target.at[spin], small_sem.at[place, spin]
        )
        for place, (target, pair_of) in enumerate(
            (
                (amp, (same_amp_ref, opposite_amp_ref)),
                (energy, (same_energy_ref, opposite_energy_ref)),
            )
        )
        for spin, source in enumerate(pair_of)
    ]
    for copy in small_copies:
        copy.start()
    for spin in range(2):
        for pair in range(count):
            pltpu.make_async_copy(
                sources[spin].at[pair], held[spin].at[pair], panel_sem.at[spin, pair]
            ).start()
    for copy in small_copies:
        copy.wait()
    share = jnp.where(places[1] == 0, 1.0, 0.0)
    for spin, ranks in enumerate((same_ranks, opposite_ranks)):
        for pair in range(count):
            keep = mask(ranks[start + pair], slots)
            value = jnp.where(keep, amp[spin, pair].astype(jnp.float32), 0.0)
            masked[spin, pair] = value.astype(jnp.bfloat16)
            gaps = energy[spin, pair]
            first = jnp.broadcast_to(gaps[0:1], (slots, slots)).T
            base_ref[spin, pair] = (first + gaps[1:2]) * value * share
    total[...] = jnp.zeros_like(total)
    for spin in range(2):
        panels = held[spin]

        @pl.loop(0, count)
        def _(pair):
            pltpu.make_async_copy(
                sources[spin].at[pair], panels.at[pair], panel_sem.at[spin, pair]
            ).wait()
            weights = masked[spin, pair]
            exchange = jnp.zeros((slots, slots), jnp.float32)
            for at, size in pieces(functions, STEP):
                left = panels[pair, 0, :, at : at + size]
                right = panels[pair, 1, :, at : at + size]
                mixed = jnp.dot(weights, right, preferred_element_type=jnp.float32)
                part = left.astype(jnp.float32) * mixed
                total[:, at : at + size] += jnp.sum(part.reshape(slots // 8, 8, size), axis=0)
                exchange += lax.dot_general(
                    left, right, ROW_BY_ROW, preferred_element_type=jnp.float32
                )
            base_ref[spin, pair] += exchange

    coupling_ref[...] = jnp.sum(total[...], axis=0, keepdims=True)


def coulomb_kernel(
    places,
    same_ranks,
    opposite_ranks,
    same_held,
    opposite_held,
    base_ref,
    *rest,
    partners,
    group,
):
    couplings, outs = rest[:partners], rest[partners:-3]
    coupling, finished, whole = rest[-3:]
    count, _, slots, functions = same_held.shape
    start, pair_index, owner = places[0], places[1], places[2]
    coupling[...] = functools.reduce(jnp.add, [ref[...] for ref in couplings])
    for spin, (panels, ranks) in enumerate(
        ((same_held, same_ranks), (opposite_held, opposite_ranks))
    ):

        @pl.loop(0, count)
        def _(pair):
            summed = jnp.zeros((slots, slots), jnp.float32)
            for at, size in pieces(functions, STEP):
                left = panels[pair, 0, :, at : at + size].astype(jnp.float32)
                scaled = (left * coupling[:, at : at + size]).astype(jnp.bfloat16)
                right = panels[pair, 1, :, at : at + size]
                summed += lax.dot_general(
                    scaled, right, ROW_BY_ROW, preferred_element_type=jnp.float32
                )
            keep = mask(ranks[start + pair], slots)
            finished[spin, pair] = jnp.where(keep, summed + base_ref[spin, pair], 0.0)

    for spin in range(2):
        for pair in range(count):
            whole[:, spin * count + pair, :] = finished[spin, pair]
    rows = slots // len(outs)
    for k, out in enumerate(outs):
        at = (pair_index ^ k ^ owner) * rows
        out[...] = whole[pl.ds(at, rows)]


def add_kernel(same_held, opposite_held, *refs):
    refs[-1][...] = functools.reduce(jnp.add, [ref[...] for ref in refs[:-1]])


def gather_kernel(places, *rest, partners, group):
    parts, outs = rest[:partners], rest[partners:-1]
    summed = rest[-1]
    summed[...] = functools.reduce(jnp.add, [ref[...] for ref in parts])
    rows = outs[0].shape[0]
    for k, out in enumerate(outs):
        out[...] = summed[pl.ds(lax.rem(places[3] + k, group) * rows, rows)]


def last_kernel(places, *rest, group):
    parts, outs = rest[:group], rest[group:]
    count = parts[0].shape[1] // 2
    values = [ref[...] for ref in parts]
    for j in range(group):
        value = values[0]
        for k in range(1, group):
            value = jnp.where(lax.rem(j + k, group) == places[3], values[k], value)
        for spin, out in enumerate(outs):
            out[:, j * count : (j + 1) * count, :] = value[:, spin * count : (spin + 1) * count, :]


def body(
    same_panels,
    opposite_panels,
    same_amplitudes,
    opposite_amplitudes,
    same_energies,
    opposite_energies,
    same_ranks,
    opposite_ranks,
):
    count, _, slots, functions = same_panels.shape
    pairs, auxes = lax.axis_size("pair"), lax.axis_size("aux")
    pair_index, aux_index = lax.axis_index("pair"), lax.axis_index("aux")
    group = auxes // pairs
    rows = slots // auxes
    f32 = jnp.float32
    places = jnp.stack(
        [aux_index * count, pair_index, aux_index // group, aux_index % group]
    ).astype(jnp.int32)
    same_held, opposite_held, coupling, base = call(
        dressing_kernel,
        (
            (same_panels.shape, same_panels.dtype),
            (opposite_panels.shape, opposite_panels.dtype),
            ((1, functions), f32),
            ((2, count, slots, slots), f32),
        ),
        [(SCALARS, places), (SCALARS, same_ranks), (SCALARS, opposite_ranks)]
        + [
            (ANYWHERE, value)
            for value in (
                same_panels,
                opposite_panels,
                same_amplitudes,
                opposite_amplitudes,
                same_energies,
                opposite_energies,
            )
        ],
        [
            pltpu.VMEM((2, count, slots, slots), jnp.bfloat16),
            pltpu.VMEM((2, count, 2, slots), f32),
            pltpu.VMEM((2, count, slots, slots), jnp.bfloat16),
            pltpu.VMEM((8, functions), f32),
            pltpu.SemaphoreType.DMA((2, count)),
            pltpu.SemaphoreType.DMA((2, 2)),
        ],
        flops=8 * count * slots * slots * functions,
        name="dressing",
    )

    def swapped(value, k):
        return lax.ppermute(value, "aux", [(i, i ^ k) for i in range(auxes)])

    (coupling,) = call(
        add_kernel,
        (((1, functions), f32),),
        [
            (ON_CHIP, value)
            for value in (same_held, opposite_held, coupling, swapped(coupling, 1))
        ],
        name="chip_sum",
    )
    couplings = [coupling] + [swapped(coupling, k) for k in range(2, auxes, 2)]
    leaving = call(
        functools.partial(coulomb_kernel, partners=len(couplings), group=group),
        (((group * rows, 2 * count, slots), f32),) * pairs,
        [(SCALARS, places), (SCALARS, same_ranks), (SCALARS, opposite_ranks)]
        + [(ON_CHIP, value) for value in (same_held, opposite_held, base, *couplings)],
        [
            pltpu.VMEM((1, functions), f32),
            pltpu.VMEM((2, count, slots, slots), f32),
            pltpu.VMEM((slots, 2 * count, slots), f32),
        ],
        flops=4 * count * slots * slots * functions,
        name="coulomb",
    )
    parts = [leaving[0]] + [
        lax.ppermute(leaving[k], "pair", [(i, i ^ k) for i in range(pairs)])
        for k in range(1, pairs)
    ]
    moving = call(
        functools.partial(gather_kernel, partners=pairs, group=group),
        (((rows, 2 * count, slots), f32),) * group,
        [(SCALARS, places)] + [(ON_CHIP, value) for value in parts],
        [pltpu.VMEM((group * rows, 2 * count, slots), f32)],
        name="pair_sum",
    )
    arrived = []
    for k in range(group):
        moves = [
            (
                p * auxes + q,
                (q // group) * auxes + group * (p ^ (q // group)) + (q % group + k) % group,
            )
            for p in range(pairs)
            for q in range(auxes)
        ]
        arrived.append(lax.ppermute(moving[k], ("pair", "aux"), moves))
    outs = pl.pallas_call(
        functools.partial(last_kernel, group=group),
        out_shape=(jax.ShapeDtypeStruct((rows, group * count, slots), f32),) * 2,
        in_specs=[SCALARS] + [ON_CHIP] * group,
        out_specs=(ON_CHIP, ON_CHIP),
        name="residual_rows",
    )(places, *(pltpu.with_memory_space_constraint(value, pltpu.VMEM) for value in arrived))
    return tuple(out.transpose(1, 0, 2) for out in outs)


def solution(mesh):
    placed = (
        P("aux", None, None, "pair"),
        P("aux", None, None, "pair"),
        P(),
        P(),
        P(),
        P(),
        P(),
        P(),
    )
    return jax.shard_map(
        body,
        mesh=mesh,
        in_specs=placed,
        out_specs=(P("pair", "aux", None), P("pair", "aux", None)),
        check_vma=False,
    )
```

time: 179 us -> 72.9 us (0.41)
  the two profiles are of different devices: /device:TPU:0 before, /device:TPU:25 now
where the time goes in v1:
time: 72.9 us; the launch traced here: 72.7 us
  Pallas kernels  42.2 us (58%)
  waiting for transfers between devices  15.5 us (21%)
  starting transfers between devices  13.7 us (19%)
    pallas_call x4, Pallas kernels, call(): pl.pallas_call(kernel, out_shape=tuple((pltpu.VMEM(shape, dtype) for shap...  40.9 us
    ppermute x2, starting transfers between devices, body(): arrived.append(lax.ppermute(moving[k], ('pair', 'aux'), moves))  6.61 us
    ppermute x2, waiting for transfers between devices, body(): arrived.append(lax.ppermute(moving[k], ('pair', 'aux'), moves))  6.15 us
    ppermute x3, waiting for transfers between devices, body(): lax.ppermute(leaving[k], 'pair', [(i, i ^ k) for i in range(pairs)])  4.93 us
    ppermute x4, waiting for transfers between devices, swapped(): return lax.ppermute(value, 'aux', [(i, i ^ k) for i in range(auxes)])  4.46 us
    ppermute x4, starting transfers between devices, swapped(): return lax.ppermute(value, 'aux', [(i, i ^ k) for i in range(auxes)])  4.34 us
    ppermute x3, starting transfers between devices, body(): lax.ppermute(leaving[k], 'pair', [(i, i ^ k) for i in range(pairs)])  2.71 us
  transfers between devices with their start and end apart: 9, of which 9 were waited for; matrix products, arithmetic and copies ran while one was open for 0% of the time, Pallas kernels for 0%

profile of v1, /device:TPU:25, one launch (start us, length us, event | category | flops | bytes accessed | tf_op | source)
XLA Modules:
  0.0 72.7 jit_solution(12421506366552680561)
XLA Ops:
  0.6 0.7 pad_add_fusion.places
  1.3 30.6 %dressing.1 = (bf16[4,2,112,14976]{3,2,1,0:T(8,128)(2,1)S(1)}, bf16[4,2,112,14976]{3,2,1,0:T(8,128)(2,1)S(1)}, f32[1,14976]{1,0:T(1,128)S(1)}, f32[2,4,112,112]{3,2,1,0:T(8,128)S(1)}) custom-call(s32[4]{0:T(128)} %pad_add_fusion.places, s32[32]{0:T(128)} %same_ranks.3, s32[32]{0:T(128)} %opposite_ranks.3, bf16[4,2,112,14976]{3,2,1,0:T(8,128)(2,1)} %same_ref.1, ...), custom_call_target="tpu_custom_call" | custom-call | flops 6011486208 | tf_op jit(solution)/shard_map/dressing/pallas_call | solution.py:28
  31.9 0.7 %collective-permute-start = (f32[1,14976]{1,0:T(1,128)S(1)}, f32[1,14976]{1,0:T(1,128)S(1)}, u32[]{:S(2)}, u32[]{:S(2)}) collective-permute-start(f32[1,14976]{1,0:T(1,128)S(1)} %get-tuple-element.17.refs_0_), channel_id=1, source_target_pairs={{0,1},{1,0},{2,3},{3,2},{4,5},{5,4},{6,7},{7,6},{8,9},{9,8},{10,11... | collective-permute-start | bytes 179720 | tf_op jit(solution)/shard_map/ppermute | solution.py:245
  32.7 0.9 %collective-permute-done.refs_1_ = f32[1,14976]{1,0:T(1,128)S(1)} collective-permute-done((f32[1,14976]{1,0:T(1,128)S(1)}, f32[1,14976]{1,0:T(1,128)S(1)}, u32[]{:S(2)}, u32[]{:S(2)}) %collective-permute-start) | collective-permute-done | bytes 59936 | tf_op jit(solution)/shard_map/ppermute | solution.py:245
  33.6 0.1 collective-permute-start.3
  33.7 1.3 %collective-permute-start.2 = (f32[1,14976]{1,0:T(1,128)S(1)}, f32[1,14976]{1,0:T(1,128)S(1)}, u32[]{:S(2)}, u32[]{:S(2)}) collective-permute-start(f32[1,14976]{1,0:T(1,128)S(1)} %chip_sum.1.rest_0_), channel_id=1, source_target_pairs={{0,4},{1,5},{2,6},{3,7},{4,0},{5,1},{6,2},{7,3},{8,12},{9,13},{10,... | collective-permute-start | bytes 179720 | tf_op jit(solution)/shard_map/ppermute | solution.py:245
  35.0 2.2 %collective-permute-start.1 = (f32[1,14976]{1,0:T(1,128)S(1)}, f32[1,14976]{1,0:T(1,128)S(1)}, u32[]{:S(2)}, u32[]{:S(2)}) collective-permute-start(f32[1,14976]{1,0:T(1,128)S(1)} %chip_sum.1.rest_0_), channel_id=1, source_target_pairs={{0,2},{1,3},{2,0},{3,1},{4,6},{5,7},{6,4},{7,5},{8,10},{9,11},{10,... | collective-permute-start | bytes 179720 | tf_op jit(solution)/shard_map/ppermute | solution.py:245
  37.2 1.4 %collective-permute-done.3.rest_3_ = f32[1,14976]{1,0:T(1,128)S(1)} collective-permute-done((f32[1,14976]{1,0:T(1,128)S(1)}, f32[1,14976]{1,0:T(1,128)S(1)}, u32[]{:S(2)}, u32[]{:S(2)}) %collective-permute-start.3) | collective-permute-done | bytes 59936 | tf_op jit(solution)/shard_map/ppermute | solution.py:245
  38.7 2.0 %collective-permute-done.2.rest_2_ = f32[1,14976]{1,0:T(1,128)S(1)} collective-permute-done((f32[1,14976]{1,0:T(1,128)S(1)}, f32[1,14976]{1,0:T(1,128)S(1)}, u32[]{:S(2)}, u32[]{:S(2)}) %collective-permute-start.2) | collective-permute-done | bytes 59936 | tf_op jit(solution)/shard_map/ppermute | solution.py:245
  40.6 0.2 collective-permute-done.1.rest_1_
  40.8 0.0 copy-start
  40.8 9.6 %coulomb.1 = (f32[28,8,112]{2,1,0:T(8,128)S(1)}, f32[28,8,112]{2,1,0:T(8,128)S(1)}, f32[28,8,112]{2,1,0:T(8,128)S(1)}, f32[28,8,112]{2,1,0:T(8,128)S(1)}) custom-call(s32[4]{0:T(128)} %pad_add_fusion.places, s32[32]{0:T(128)} %same_ranks.3, s32[32]{0:T(128)} %opposite_ranks.3, bf16[4,2,112,14976]{3,2,1,0:T(8,128)(2,1)S(1)} %get-tuple-element.14.same_held, ...), custom_call_target="tpu_custom_call" | custom-call | flops 3005743104 | tf_op jit(solution)/shard_map/coulomb/pallas_call | solution.py:28
  50.4 1.3 %collective-permute-start.4 = (f32[28,8,112]{2,1,0:T(8,128)S(1)}, f32[28,8,112]{2,1,0:T(8,128)S(1)}, u32[]{:S(2)}, u32[]{:S(2)}) collective-permute-start(f32[28,8,112]{2,1,0:T(8,128)S(1)} %get-tuple-element.19), channel_id=1, source_target_pairs={{0,8},{8,0},{16,24},{24,16},{1,9},{9,1},{17,25},{25,17},{2,10},{10... | collective-permute-start | bytes 301064 | tf_op jit(solution)/shard_map/ppermute | solution.py:271
  51.7 1.2 %collective-permute-start.5 = (f32[28,8,112]{2,1,0:T(8,128)S(1)}, f32[28,8,112]{2,1,0:T(8,128)S(1)}, u32[]{:S(2)}, u32[]{:S(2)}) collective-permute-start(f32[28,8,112]{2,1,0:T(8,128)S(1)} %get-tuple-element.20), channel_id=1, source_target_pairs={{0,16},{8,24},{16,0},{24,8},{1,17},{9,25},{17,1},{25,9},{2,18},{10... | collective-permute-start | bytes 301064 | tf_op jit(solution)/shard_map/ppermute | solution.py:271
  52.9 0.2 collective-permute-start.6
  53.1 1.0 %collective-permute-done.4.rest_1_ = f32[28,8,112]{2,1,0:T(8,128)S(1)} collective-permute-done((f32[28,8,112]{2,1,0:T(8,128)S(1)}, f32[28,8,112]{2,1,0:T(8,128)S(1)}, u32[]{:S(2)}, u32[]{:S(2)}) %collective-permute-start.4) | collective-permute-done | bytes 100384 | tf_op jit(solution)/shard_map/ppermute | solution.py:271
  54.1 1.5 %collective-permute-done.5.rest_2_ = f32[28,8,112]{2,1,0:T(8,128)S(1)} collective-permute-done((f32[28,8,112]{2,1,0:T(8,128)S(1)}, f32[28,8,112]{2,1,0:T(8,128)S(1)}, u32[]{:S(2)}, u32[]{:S(2)}) %collective-permute-start.5) | collective-permute-done | bytes 100384 | tf_op jit(solution)/shard_map/ppermute | solution.py:271
  55.6 2.4 %collective-permute-done.6.rest_3_ = f32[28,8,112]{2,1,0:T(8,128)S(1)} collective-permute-done((f32[28,8,112]{2,1,0:T(8,128)S(1)}, f32[28,8,112]{2,1,0:T(8,128)S(1)}, u32[]{:S(2)}, u32[]{:S(2)}) %collective-permute-start.6) | collective-permute-done | bytes 100384 | tf_op jit(solution)/shard_map/ppermute | solution.py:271
  58.1 0.0 copy-done
  58.1 0.6 pair_sum.1
  58.6 2.6 %collective-permute-start.7 = (f32[14,8,112]{2,1,0:T(8,128)S(1)}, f32[14,8,112]{2,1,0:T(8,128)S(1)}, u32[]{:S(2)}, u32[]{:S(2)}) collective-permute-start(f32[14,8,112]{2,1,0:T(8,128)S(1)} %get-tuple-element.22), channel_id=1, source_target_pairs={{0,0},{1,1},{2,10},{3,11},{4,20},{5,21},{6,30},{7,31},{8,2},{9,3},... | collective-permute-start | bytes 150536 | tf_op jit(solution)/shard_map/ppermute | solution.py:291
  61.2 4.1 %collective-permute-start.8 = (f32[14,8,112]{2,1,0:T(8,128)S(1)}, f32[14,8,112]{2,1,0:T(8,128)S(1)}, u32[]{:S(2)}, u32[]{:S(2)}) collective-permute-start(f32[14,8,112]{2,1,0:T(8,128)S(1)} %get-tuple-element.23), channel_id=1, source_target_pairs={{0,1},{1,0},{2,11},{3,10},{4,21},{5,20},{6,31},{7,30},{8,3},{9,2},... | collective-permute-start | bytes 150536 | tf_op jit(solution)/shard_map/ppermute | solution.py:291
  65.3 1.9 %collective-permute-done.7.rest_0_ = f32[14,8,112]{2,1,0:T(8,128)S(1)} collective-permute-done((f32[14,8,112]{2,1,0:T(8,128)S(1)}, f32[14,8,112]{2,1,0:T(8,128)S(1)}, u32[]{:S(2)}, u32[]{:S(2)}) %collective-permute-start.7) | collective-permute-done | bytes 50208 | tf_op jit(solution)/shard_map/ppermute | solution.py:291
  67.2 4.2 %collective-permute-done.8.rest_1_ = f32[14,8,112]{2,1,0:T(8,128)S(1)} collective-permute-done((f32[14,8,112]{2,1,0:T(8,128)S(1)}, f32[14,8,112]{2,1,0:T(8,128)S(1)}, u32[]{:S(2)}, u32[]{:S(2)}) %collective-permute-start.8) | collective-permute-done | bytes 50208 | tf_op jit(solution)/shard_map/ppermute | solution.py:291
  71.4 1.3 %residual_rows.1 = (f32[14,8,112]{2,1,0:T(8,128)}, f32[14,8,112]{2,1,0:T(8,128)}) custom-call(s32[4]{0:T(128)} %pad_add_fusion.places, f32[14,8,112]{2,1,0:T(8,128)S(1)} %collective-permute-done.7.rest_0_, f32[14,8,112]{2,1,0:T(8,128)S(1)} %collective-permute-done.8.rest_1_), custom_call_target="tpu_custom_call" | custom-call | tf_op jit(solution)/shard_map/residual_rows/pallas_call | solution.py:292
  (1 shorter events, 0.0 us)
Async XLA Ops:
  31.9 1.6 %collective-permute-start = (f32[1,14976]{1,0:T(1,128)S(1)}, f32[1,14976]{1,0:T(1,128)S(1)}, u32[]{:S(2)}, u32[]{:S(2)}) collective-permute-start(f32[1,14976]{1,0:T(1,128)S(1)} %get-tuple-element.17.refs_0_), channel_id=1, source_target_pairs={{0,1},{1,0},{2,3},{3,2},{4,5},{5,4},{6,7},{7,6},{8,9},{9,8},{10,11... | collective-permute-start | bytes 179720 | tf_op jit(solution)/shard_map/ppermute | solution.py:245
  33.6 5.1 %collective-permute-start.3 = (f32[1,14976]{1,0:T(1,128)S(1)}, f32[1,14976]{1,0:T(1,128)S(1)}, u32[]{:S(2)}, u32[]{:S(2)}) collective-permute-start(f32[1,14976]{1,0:T(1,128)S(1)} %chip_sum.1.rest_0_), channel_id=1, source_target_pairs={{0,6},{1,7},{2,4},{3,5},{4,2},{5,3},{6,0},{7,1},{8,14},{9,15},{10,... | collective-permute-start | bytes 179720 | tf_op jit(solution)/shard_map/ppermute | solution.py:245
  33.7 6.9 %collective-permute-start.2 = (f32[1,14976]{1,0:T(1,128)S(1)}, f32[1,14976]{1,0:T(1,128)S(1)}, u32[]{:S(2)}, u32[]{:S(2)}) collective-permute-start(f32[1,14976]{1,0:T(1,128)S(1)} %chip_sum.1.rest_0_), channel_id=1, source_target_pairs={{0,4},{1,5},{2,6},{3,7},{4,0},{5,1},{6,2},{7,3},{8,12},{9,13},{10,... | collective-permute-start | bytes 179720 | tf_op jit(solution)/shard_map/ppermute | solution.py:245
  35.0 5.8 %collective-permute-start.1 = (f32[1,14976]{1,0:T(1,128)S(1)}, f32[1,14976]{1,0:T(1,128)S(1)}, u32[]{:S(2)}, u32[]{:S(2)}) collective-permute-start(f32[1,14976]{1,0:T(1,128)S(1)} %chip_sum.1.rest_0_), channel_id=1, source_target_pairs={{0,2},{1,3},{2,0},{3,1},{4,6},{5,7},{6,4},{7,5},{8,10},{9,11},{10,... | collective-permute-start | bytes 179720 | tf_op jit(solution)/shard_map/ppermute | solution.py:245
  40.8 17.3 %copy-start = (s32[4]{0:T(128)S(1)}, s32[4]{0:T(128)}, u32[]{:S(2)}) copy-start(s32[4]{0:T(128)} %pad_add_fusion.places) | copy-start | bytes 52
  50.4 3.7 %collective-permute-start.4 = (f32[28,8,112]{2,1,0:T(8,128)S(1)}, f32[28,8,112]{2,1,0:T(8,128)S(1)}, u32[]{:S(2)}, u32[]{:S(2)}) collective-permute-start(f32[28,8,112]{2,1,0:T(8,128)S(1)} %get-tuple-element.19), channel_id=1, source_target_pairs={{0,8},{8,0},{16,24},{24,16},{1,9},{9,1},{17,25},{25,17},{2,10},{10... | collective-permute-start | bytes 301064 | tf_op jit(solution)/shard_map/ppermute | solution.py:271
  51.7 3.9 %collective-permute-start.5 = (f32[28,8,112]{2,1,0:T(8,128)S(1)}, f32[28,8,112]{2,1,0:T(8,128)S(1)}, u32[]{:S(2)}, u32[]{:S(2)}) collective-permute-start(f32[28,8,112]{2,1,0:T(8,128)S(1)} %get-tuple-element.20), channel_id=1, source_target_pairs={{0,16},{8,24},{16,0},{24,8},{1,17},{9,25},{17,1},{25,9},{2,18},{10... | collective-permute-start | bytes 301064 | tf_op jit(solution)/shard_map/ppermute | solution.py:271
  52.9 5.1 %collective-permute-start.6 = (f32[28,8,112]{2,1,0:T(8,128)S(1)}, f32[28,8,112]{2,1,0:T(8,128)S(1)}, u32[]{:S(2)}, u32[]{:S(2)}) collective-permute-start(f32[28,8,112]{2,1,0:T(8,128)S(1)} %get-tuple-element.21), channel_id=1, source_target_pairs={{0,24},{8,16},{16,8},{24,0},{1,25},{9,17},{17,9},{25,1},{2,26},{10... | collective-permute-start | bytes 301064 | tf_op jit(solution)/shard_map/ppermute | solution.py:271
  58.6 8.6 %collective-permute-start.7 = (f32[14,8,112]{2,1,0:T(8,128)S(1)}, f32[14,8,112]{2,1,0:T(8,128)S(1)}, u32[]{:S(2)}, u32[]{:S(2)}) collective-permute-start(f32[14,8,112]{2,1,0:T(8,128)S(1)} %get-tuple-element.22), channel_id=1, source_target_pairs={{0,0},{1,1},{2,10},{3,11},{4,20},{5,21},{6,30},{7,31},{8,2},{9,3},... | collective-permute-start | bytes 150536 | tf_op jit(solution)/shard_map/ppermute | solution.py:291
  61.2 10.2 %collective-permute-start.8 = (f32[14,8,112]{2,1,0:T(8,128)S(1)}, f32[14,8,112]{2,1,0:T(8,128)S(1)}, u32[]{:S(2)}, u32[]{:S(2)}) collective-permute-start(f32[14,8,112]{2,1,0:T(8,128)S(1)} %get-tuple-element.23), channel_id=1, source_target_pairs={{0,1},{1,0},{2,11},{3,10},{4,21},{5,20},{6,31},{7,30},{8,3},{9,2},... | collective-permute-start | bytes 150536 | tf_op jit(solution)/shard_map/ppermute | solution.py:291
